TPU v7x, 32 devices: a whole 2x2x4 slice. The times are simulated.
32 devices in a mesh: dp: 4 (over y, core), vocab: 8 (over z, x).
Axes of the slice: x: 2, y: 2, z: 4, core: 2. Of those that a mesh axis runs over, the one named last changes fastest.
Arguments:
- hidden: bfloat16 [256, 3584], P('dp'), may hold values from -48 to 48
- embedding: bfloat16 [24576, 3584], P(('dp', 'vocab')), may hold values from -1 to 1
- targets: int32 [256], P('dp'), may hold values from 0 to 24575
- loss_weight: bfloat16 [256], P('dp'), may hold values from 1 to 10
Outputs:
- hidden_grad: bfloat16 [256, 3584], P('dp')
- table_grad: bfloat16 [24576, 3584], P(('dp', 'vocab'))
All inputs are finite; a program needn't handle non-finite values.
Results may differ from a plain program's by a relative error of at most 0.0049.
Values may be sent and summed in bfloat16 or wider, within the bound.
A program may use at most 128 MiB of HBM per device.

v0:
```python
import jax
import jax.numpy as jnp
from jax import lax
from jax.sharding import PartitionSpec as P

soft_cap = 30.0
z_weight = 0.002


def body(hidden, embedding, targets, loss_weight):
    shard_rows = embedding.shape[0]
    group_hidden, group_weight = (
        lax.all_gather(hidden, "dp", axis=0, tiled=True),
        lax.all_gather(loss_weight, "dp", axis=0, tiled=True),
    )
    group_targets = lax.all_gather(targets, "dp", axis=0, tiled=True)
    logits = lax.dot_general(
        group_hidden, embedding, (((1,), (1,)), ((), ())), preferred_element_type=jnp.float32
    )
    capped = soft_cap * jnp.tanh(logits / soft_cap)
    exp_terms = jnp.exp(capped - soft_cap)
    partial_value = jnp.sum(exp_terms, axis=1)
    weight = group_weight.astype(jnp.float32)
    device_place = lax.axis_index("dp") * lax.axis_size("vocab") + lax.axis_index("vocab")
    exp_total = lax.psum(partial_value, ("dp", "vocab"))
    factor = weight * (1.0 + 2.0 * z_weight * (soft_cap + jnp.log(exp_total))) / exp_total
    columns = device_place * shard_rows + lax.iota(jnp.int32, shard_rows)
    target_hit = group_targets[:, None] == columns[None, :]
    softmax_part = factor[:, None] * exp_terms - jnp.where(target_hit, weight[:, None], 0.0)
    scores_grad = (softmax_part * (1.0 - (capped / soft_cap) ** 2)).astype(jnp.bfloat16)
    table_grad = lax.dot_general(
        scores_grad, group_hidden, (((0,), (0,)), ((), ())), preferred_element_type=jnp.float32
    ).astype(jnp.bfloat16)
    group_grad = lax.psum_scatter(
        jnp.dot(scores_grad, embedding, preferred_element_type=jnp.float32),
        "dp",
        scatter_dimension=0,
        tiled=True,
    )
    hidden_grad = lax.psum(group_grad, "vocab").astype(jnp.bfloat16)
    return (hidden_grad, table_grad)


def solution(mesh):
    return jax.shard_map(
        body,
        mesh=mesh,
        in_specs=(P("dp", None), P(("dp", "vocab"), None), P("dp"), P("dp")),
        out_specs=(P("dp", None), P(("dp", "vocab"), None)),
        check_vma=False,
    )
```

profile of v0, /device:TPU:0, one launch (start us, length us, event | category | flops | bytes accessed | tf_op | source)
XLA Modules:
  0.0 182.5 jit_solution(10813239611045289594)
XLA Ops:
  7.2 0.0 all-gather.2.cloned.1.call-start
  7.2 0.7 all-gather.2.cloned.1.call-update
  7.9 0.0 reduce-scatter.2.cloned.1.call-start
  8.0 1.2 dynamic-slice
  9.9 0.9 dynamic-update-slice
  10.7 8.4 %all-reduce = bf16[256]{0:T(256)(128)(2,1)S(1)} all-reduce(bf16[256]{0:T(256)(128)(2,1)S(1)} %dynamic-update-slice), channel_id=1, replica_groups=mesh['dp'=4,'vocab'=8] {'dp'}, use_global_device_ids=true, to_apply=%add | all-reduce | flops 256 | bytes 1024
  19.1 0.9 dynamic-update-slice.1
  20.0 4.5 %all-reduce.1 = s32[256]{0:T(256)S(1)} all-reduce(s32[256]{0:T(256)S(1)} %dynamic-update-slice.1), channel_id=1, replica_groups=mesh['dp'=4,'vocab'=8] {'dp'}, use_global_device_ids=true, to_apply=%add.1 | all-reduce | flops 256 | bytes 2048
  24.4 9.0 %all-gather.2.cloned.1.call-done = bf16[256,3584]{1,0:T(8,128)(2,1)} async-done(((bf16[64,3584]{1,0:T(8,128)(2,1)}), bf16[256,3584]{1,0:T(8,128)(2,1)}) %all-gather.2.cloned.1.call-update) | async-done | bytes 1835024 | tf_op jit(solution)/shard_map/all_gather | solution.py:13
  33.5 4.9 %fusion.1 = (f32[256]{0:T(256)S(1)}, f32[256,768]{1,0:T(8,128)S(1)}) fusion(bf16[256,3584]{1,0:T(8,128)(2,1)} %all-gather.2.cloned.1.call-done, bf16[768,3584]{1,0:T(8,128)(2,1)} %param.5), kind=kOutput, calls=%fused_computation.5 | convolution fusion | flops 1410072320 | bytes 8127488 | tf_op jit(solution)/shard_map/dot_general | solution.py:17
  38.4 39.3 %psum.14 = f32[256]{0:T(256)S(1)} all-reduce(f32[256]{0:T(256)S(1)} %get-tuple-element.2), channel_id=1, replica_groups=mesh['dp'=4,'vocab'=8] {'dp','vocab'}, use_global_device_ids=true, to_apply=%region_1.0 | all-reduce | flops 256 | bytes 2048 | tf_op jit(solution)/shard_map/psum | solution.py:25
  77.7 0.0 copy-start
  77.7 6.3 %fusion.2 = f32[256,3584]{1,0:T(8,128)} fusion(bf16[768,3584]{1,0:T(8,128)(2,1)} %param.5, f32[256,768]{1,0:T(8,128)S(1)} %get-tuple-element.3, f32[256]{0:T(256)S(1)} %convert_element_type.12, s32[768]{0:T(1024)S(1)} %iota_add_fusion, f32[256]{0:T(256)S(1)} %multiply_divide_fusion, s32[256]{0:T(256)S(1)} %all-reduce.1), kind=kOutput, calls=%fused_computation.8 | convolution fusion | flops 1411252224 | bytes 9967616 | tf_op jit(solution)/shard_map/dot_general | solution.py:35
  84.0 0.0 reduce-scatter.2.cloned.1.call-update
  84.0 0.0 copy-done
  84.0 4.3 %convolution_convert_fusion = bf16[768,3584]{1,0:T(8,128)(2,1)} fusion(bf16[256,3584]{1,0:T(8,128)(2,1)S(1)} %copy-done, f32[256,768]{1,0:T(8,128)S(1)} %get-tuple-element.3, f32[256]{0:T(256)S(1)} %convert_element_type.12, s32[768]{0:T(1024)S(1)} %iota_add_fusion, f32[256]{0:T(256)S(1)} %multiply_divide_fusion, s32[256]{0:T(256)S(1)} %all-reduce.1), kind=kOutput, calls=%fused_computation | convolution fusion | flops 1414004736 | bytes 8132608 | tf_op jit(solution)/shard_map/dot_general | solution.py:31
  88.3 37.9 %reduce-scatter.2.cloned.1.call-done = f32[64,3584]{1,0:T(8,128)} async-done(((f32[256,3584]{1,0:T(8,128)}), f32[64,3584]{1,0:T(8,128)}) %reduce-scatter.2.cloned.1.call-update) | async-done | bytes 917520 | tf_op jit(solution)/shard_map/reduce_scatter | solution.py:34
  126.2 49.4 %all-reduce.3 = bf16[64,3584]{1,0:T(8,128)(2,1)} all-reduce(f32[64,3584]{1,0:T(8,128)} %reduce-scatter.2.cloned.1.call-done), channel_id=1, replica_groups=mesh['dp'=4,'vocab'=8] {'vocab'}, use_global_device_ids=true, to_apply=%region_3.4 | all-reduce | flops 229376 | bytes 1376256 | tf_op jit(solution)/shard_map/psum | solution.py:40
  (5 shorter events, 0.0 us)
Async XLA Ops:
  7.2 26.3 %all-gather.2.cloned.1.call-start = ((), (), s32[]{:S(2)}) async-start(), calls=%async_computation.1 | async-start | bytes 2293760 | tf_op jit(solution)/shard_map/all_gather | solution.py:13
  7.9 118.3 %reduce-scatter.2.cloned.1.call-start = ((), (), s32[]{:S(2)}) async-start(), calls=%async_computation.2 | async-start | bytes 4587520 | tf_op jit(solution)/shard_map/reduce_scatter | solution.py:34
  77.7 6.3 %copy-start = (bf16[256,3584]{1,0:T(8,128)(2,1)S(1)}, bf16[256,3584]{1,0:T(8,128)(2,1)}, u32[]{:S(2)}) copy-start(bf16[256,3584]{1,0:T(8,128)(2,1)} %all-gather.2.cloned.1.call-done) | copy-start | bytes 5505028
Sparse Core Ops, SparseCore 0:
  9.5 23.9 all-gather.1
  84.1 42.0 reduce-scatter.1
where the time goes:
time: 183 us; the launch traced here: 182 us
  blocking collectives  102 us (56%)
  waiting for transfers between devices  47.6 us (26%)
  matrix products  15.4 us (8%)
  between operations  14.7 us (8%)
  local copies, waits for them, and re-layouts  2.97 us (2%)
    psum x1, blocking collectives, body(): hidden_grad = lax.psum(group_grad, 'vocab').astype(jnp.bfloat16)  49.4 us
    psum x1, blocking collectives, body(): exp_total = lax.psum(partial_value, ('dp', 'vocab'))  39.3 us
    reduce_scatter x1, waiting for transfers between devices, body(): lax.psum_scatter(jnp.dot(scores_grad, embedding, preferred_element_type=j...  37.9 us
    unnamed x2, blocking collectives  12.8 us
    all_gather x1, waiting for transfers between devices, body(): lax.all_gather(hidden, 'dp', axis=0, tiled=True)  9.04 us
    dot_general x1, matrix products, body(): jnp.dot(scores_grad, embedding, preferred_element_type=jnp.float32)  6.28 us
    dot_general x1, matrix products, body(): lax.dot_general(group_hidden, embedding, (((1,), (1,)), ((), ())), prefer...  4.91 us
    dot_general x1, matrix products, body(): lax.dot_general(scores_grad, group_hidden, (((0,), (0,)), ((), ())), pref...  4.26 us
  transfers between devices with their start and end apart: 2, of which 2 were waited for; matrix products, arithmetic and copies ran while one was open for 4% of the time, Pallas kernels for 0%

commit v1 on v0

--- a/solution.py
+++ b/solution.py
@@ -22,7 +22,7 @@
     partial_value = jnp.sum(exp_terms, axis=1)
     weight = group_weight.astype(jnp.float32)
     device_place = lax.axis_index("dp") * lax.axis_size("vocab") + lax.axis_index("vocab")
-    exp_total = lax.psum(partial_value, ("dp", "vocab"))
+    exp_total = lax.psum(lax.psum(partial_value, "vocab"), "dp")
     factor = weight * (1.0 + 2.0 * z_weight * (soft_cap + jnp.log(exp_total))) / exp_total
     columns = device_place * shard_rows + lax.iota(jnp.int32, shard_rows)
     target_hit = group_targets[:, None] == columns[None, :]

time: 183 us -> 166 us (0.907)
  blocking collectives: 102 us -> 89.5 us
  waiting for transfers between devices: 47.6 us -> 42.8 us
    psum x1 -> x2, blocking collectives: 39.3 us -> 27.3 us  [body(): exp_total = lax.psum(lax.psum(partial_value, 'vocab'), 'dp')]
    reduce_scatter x1, waiting for transfers between devices: 37.9 us -> 33.1 us  [body(): lax.psum_scatter(jnp.dot(scores_grad, embedding, preferred_element_type=j...]
where the time goes in v1:
time: 166 us
  blocking collectives  89.5 us (54%)
  waiting for transfers between devices  42.8 us (26%)
  matrix products  15.5 us (9%)
  between operations  14.7 us (9%)
  local copies, waits for them, and re-layouts  2.97 us (2%)
    psum x1, blocking collectives, body(): hidden_grad = lax.psum(group_grad, 'vocab').astype(jnp.bfloat16)  49.4 us
    reduce_scatter x1, waiting for transfers between devices, body(): lax.psum_scatter(jnp.dot(scores_grad, embedding, preferred_element_type=j...  33.1 us
    psum x2, blocking collectives, body(): exp_total = lax.psum(lax.psum(partial_value, 'vocab'), 'dp')  27.3 us
    unnamed x2, blocking collectives  12.8 us
    all_gather x1, waiting for transfers between devices, body(): lax.all_gather(hidden, 'dp', axis=0, tiled=True)  9.04 us
    dot_general x1, matrix products, body(): jnp.dot(scores_grad, embedding, preferred_element_type=jnp.float32)  6.28 us
    dot_general x1, matrix products, body(): lax.dot_general(group_hidden, embedding, (((1,), (1,)), ((), ())), prefer...  4.91 us
    dot_general x1, matrix products, body(): lax.dot_general(scores_grad, group_hidden, (((0,), (0,)), ((), ())), pref...  4.32 us
  transfers between devices with their start and end apart: 2, of which 2 were waited for; matrix products, arithmetic and copies ran while one was open for 4% of the time, Pallas kernels for 0%

profile of v1, /device:TPU:0, one launch (start us, length us, event | category | flops | bytes accessed | tf_op | source)
XLA Modules:
  0.0 165.6 jit_solution(14732195251972896261)
XLA Ops:
  7.2 0.0 all-gather.2.cloned.1.call-start
  7.2 0.7 all-gather.2.cloned.1.call-update
  7.9 0.0 reduce-scatter.2.cloned.1.call-start
  8.0 1.2 dynamic-slice
  9.9 0.9 dynamic-update-slice
  10.7 8.4 %all-reduce = bf16[256]{0:T(256)(128)(2,1)S(1)} all-reduce(bf16[256]{0:T(256)(128)(2,1)S(1)} %dynamic-update-slice), channel_id=1, replica_groups=mesh['dp'=4,'vocab'=8] {'dp'}, use_global_device_ids=true, to_apply=%add | all-reduce | flops 256 | bytes 1024
  19.1 0.9 dynamic-update-slice.1
  20.0 4.5 %all-reduce.1 = s32[256]{0:T(256)S(1)} all-reduce(s32[256]{0:T(256)S(1)} %dynamic-update-slice.1), channel_id=1, replica_groups=mesh['dp'=4,'vocab'=8] {'dp'}, use_global_device_ids=true, to_apply=%add.1 | all-reduce | flops 256 | bytes 2048
  24.4 9.0 %all-gather.2.cloned.1.call-done = bf16[256,3584]{1,0:T(8,128)(2,1)} async-done(((bf16[64,3584]{1,0:T(8,128)(2,1)}), bf16[256,3584]{1,0:T(8,128)(2,1)}) %all-gather.2.cloned.1.call-update) | async-done | bytes 1835024 | tf_op jit(solution)/shard_map/all_gather | solution.py:13
  33.5 4.9 %fusion.1 = (f32[256]{0:T(256)S(1)}, f32[256,768]{1,0:T(8,128)S(1)}) fusion(bf16[256,3584]{1,0:T(8,128)(2,1)} %all-gather.2.cloned.1.call-done, bf16[768,3584]{1,0:T(8,128)(2,1)} %param.5), kind=kOutput, calls=%fused_computation.5 | convolution fusion | flops 1410072320 | bytes 8127488 | tf_op jit(solution)/shard_map/dot_general | solution.py:17
  38.4 21.4 %psum.21 = f32[256]{0:T(256)S(1)} all-reduce(f32[256]{0:T(256)S(1)} %get-tuple-element.2), channel_id=1, replica_groups=mesh['dp'=4,'vocab'=8] {'vocab'}, use_global_device_ids=true, to_apply=%region_1.0 | all-reduce | flops 256 | bytes 2048 | tf_op jit(solution)/shard_map/psum | solution.py:25
  59.7 5.9 %psum.22 = f32[256]{0:T(256)S(1)} all-reduce(f32[256]{0:T(256)S(1)} %psum.21), channel_id=1, replica_groups=mesh['dp'=4,'vocab'=8] {'dp'}, use_global_device_ids=true, to_apply=%region_2.0 | all-reduce | flops 256 | bytes 2048 | tf_op jit(solution)/shard_map/psum | solution.py:25
  65.7 0.0 copy-start
  65.7 6.3 %fusion.2 = f32[256,3584]{1,0:T(8,128)} fusion(bf16[768,3584]{1,0:T(8,128)(2,1)} %param.5, f32[256,768]{1,0:T(8,128)S(1)} %get-tuple-element.3, f32[256]{0:T(256)S(1)} %convert_element_type.12, s32[768]{0:T(1024)S(1)} %iota_add_fusion, f32[256]{0:T(256)S(1)} %multiply_divide_fusion, s32[256]{0:T(256)S(1)} %all-reduce.1), kind=kOutput, calls=%fused_computation.8 | convolution fusion | flops 1411252224 | bytes 9967616 | tf_op jit(solution)/shard_map/dot_general | solution.py:35
  72.0 0.0 reduce-scatter.2.cloned.1.call-update
  72.0 0.0 copy-done
  72.0 4.3 %convolution_convert_fusion = bf16[768,3584]{1,0:T(8,128)(2,1)} fusion(bf16[256,3584]{1,0:T(8,128)(2,1)S(1)} %copy-done, f32[256,768]{1,0:T(8,128)S(1)} %get-tuple-element.3, f32[256]{0:T(256)S(1)} %convert_element_type.12, s32[768]{0:T(1024)S(1)} %iota_add_fusion, f32[256]{0:T(256)S(1)} %multiply_divide_fusion, s32[256]{0:T(256)S(1)} %all-reduce.1), kind=kOutput, calls=%fused_computation | convolution fusion | flops 1414004736 | bytes 8132608 | tf_op jit(solution)/shard_map/dot_general | solution.py:31
  76.3 33.1 %reduce-scatter.2.cloned.1.call-done = f32[64,3584]{1,0:T(8,128)} async-done(((f32[256,3584]{1,0:T(8,128)}), f32[64,3584]{1,0:T(8,128)}) %reduce-scatter.2.cloned.1.call-update) | async-done | bytes 917520 | tf_op jit(solution)/shard_map/reduce_scatter | solution.py:34
  109.4 49.4 %all-reduce.3 = bf16[64,3584]{1,0:T(8,128)(2,1)} all-reduce(f32[64,3584]{1,0:T(8,128)} %reduce-scatter.2.cloned.1.call-done), channel_id=1, replica_groups=mesh['dp'=4,'vocab'=8] {'vocab'}, use_global_device_ids=true, to_apply=%region_4.5 | all-reduce | flops 229376 | bytes 1376256 | tf_op jit(solution)/shard_map/psum | solution.py:40
  (5 shorter events, 0.0 us)
Async XLA Ops:
  7.2 26.3 %all-gather.2.cloned.1.call-start = ((), (), s32[]{:S(2)}) async-start(), calls=%async_computation.1 | async-start | bytes 2293760 | tf_op jit(solution)/shard_map/all_gather | solution.py:13
  7.9 101.5 %reduce-scatter.2.cloned.1.call-start = ((), (), s32[]{:S(2)}) async-start(), calls=%async_computation.2 | async-start | bytes 4587520 | tf_op jit(solution)/shard_map/reduce_scatter | solution.py:34
  65.7 6.3 %copy-start = (bf16[256,3584]{1,0:T(8,128)(2,1)S(1)}, bf16[256,3584]{1,0:T(8,128)(2,1)}, u32[]{:S(2)}) copy-start(bf16[256,3584]{1,0:T(8,128)(2,1)} %all-gather.2.cloned.1.call-done) | copy-start | bytes 5505028
Sparse Core Ops, SparseCore 0:
  9.5 23.9 all-gather.1
  72.1 37.2 reduce-scatter.1
